TPU v7x, 128 devices: a whole 4x4x4 slice. The times are simulated.
128 devices in a mesh: wide: 32 (over z, y, x_hi), narrow: 4 (over x_lo, core).
Axes of the slice: x: 4 (x_hi: 2, x_lo: 2; x = x_hi * 2 + x_lo), y: 4, z: 4, core: 2. Of those that a mesh axis runs over, the one named last changes fastest.
Arguments:
- image_tower: bfloat16 [64, 2560, 1024], P('wide', 'narrow'), may hold values from -150 to 150
- text_tower: bfloat16 [163840, 1024], P(('wide', 'narrow')), may hold values from -150 to 150
- image_proj: bfloat16 [2, 1024, 768], replicated, may hold values from -1 to 1
- text_proj: bfloat16 [2, 1024, 768], replicated, may hold values from -1 to 1
- logit_scale: float32 [2], replicated, may hold values from 8 to 300
- pair_ids: int32 [163840], P(('wide', 'narrow')), may hold values from 0 to 163839, each once
- band_index: int32 [1], replicated, may hold values from 0 to 63
Outputs:
- learnability: float32 [2560], P('narrow')
- column_lse: float32 [2, 163840], P(None, ('wide', 'narrow'))
Inputs may be any that keep to these rules, and one draw needn't show every extreme that they name: Text t is paired with image pair_ids[t], numbered band * 2560 + position in the band; every image has exactly one text.
All inputs are finite; a program needn't handle non-finite values.
Results may differ from a plain program's by a relative error of at most 0.0041.
Values may be sent and summed in bfloat16 or wider, within the bound.
No kernel may reach another device: no remote copies, remote signals or barrier semaphores. Data moves between devices by JAX's collectives and lax.ppermute only.
A program may use at most 128 MiB of HBM per device.

v0:
```python
import jax
import jax.numpy as jnp
from jax import lax
from jax.sharding import Mesh
from jax.sharding import PartitionSpec as P

WIDE = ("wide_0", "wide_1", "wide_2")
NARROW = ("narrow_0", "narrow_1")
WIDE_NARROW = ("wide_0", "wide_1", "wide_2", "narrow_0", "narrow_1")


def filled_up(lines, size):
    spare = -lines.shape[0] % size
    if not spare:
        return lines
    return jnp.concatenate([lines, jnp.zeros((spare, *lines.shape[1:]), lines.dtype)])


def from_root(value, axis, root):
    lines = jnp.where(lax.axis_index(axis) == root, value, jnp.zeros_like(value)).reshape(
        -1, *value.shape[1:][-1:]
    )
    padded = filled_up(lines, lax.axis_size(axis))
    own = lax.psum_scatter(padded, axis, scatter_dimension=0, tiled=True)
    return lax.all_gather(own, axis, axis=0, tiled=True)[: len(lines)].reshape(value.shape)


def collected_together(value, axis):
    leaves = jax.tree.leaves(value)
    order = sorted(range(len(leaves)), key=lambda k: -leaves[k].size)
    width = (1, *leaves[order[0]].shape)[-1]
    lines = [
        jnp.pad(leaves[k].reshape(-1), (0, -leaves[k].size % width)).reshape(-1, width)
        for k in order
    ]
    both, at, found = (lax.all_gather(jnp.concatenate(lines), axis), 0, {})
    for k, line in zip(order, lines):
        share = both[:, at : at + len(line)].reshape(len(both), -1)
        found[k] = share[:, : leaves[k].size].reshape(-1, *leaves[k].shape)
        at += len(line)
    numbers = iter(range(len(leaves)))
    return jax.tree.map(lambda _: found[next(numbers)], value)


def joined_all(value, axes, combine):
    for axis in axes:
        pieces = collected_together(value, axis)
        value = jax.tree.map(lambda part: part[0], pieces)
        for k in range(1, lax.axis_size(axis)):
            value = combine(value, jax.tree.map(lambda part: part[k], pieces))
    return value


def embed(tower, weight):
    full = jnp.dot(tower, weight, preferred_element_type=jnp.float32)
    return (full * lax.rsqrt(jnp.sum(full * full, axis=-1, keepdims=True) + 1e-06)).astype(
        jnp.bfloat16
    )


def both_heads(tower, weights):
    return jnp.stack([embed(tower, weights[0]), embed(tower, weights[1])])


def join_rows(first, second):
    top = jnp.maximum(first[0], second[0])
    total = first[1] * jnp.exp(first[0] - top) + second[1] * jnp.exp(second[0] - top)
    return (top, total, first[2] + second[2])


def per_device(image_tower, text_tower, image_proj, text_proj, logit_scale, pair_ids, band_index):
    held = image_tower.shape[0]
    rows = image_tower.shape[1]
    text_count = text_tower.shape[0]
    picked = band_index[0]
    owner = picked // held
    mine = lax.dynamic_index_in_dim(image_tower, picked % held, 0, keepdims=False)
    band_rows = from_root(mine, WIDE, owner)
    band_emb = both_heads(band_rows, image_proj)
    text_emb = both_heads(text_tower, text_proj)
    scale = logit_scale[:, None, None]
    position = lax.axis_index(NARROW)
    groups = lax.axis_size(NARROW)
    band_size = rows * groups
    start_max = jnp.full((2, text_count), -1e30, jnp.float32)
    piece = lax.all_gather(band_emb, NARROW, axis=1, tiled=True)
    col_max = start_max
    count = piece.shape[1]
    logits = scale * jnp.einsum("hid,hjd->hij", piece, text_emb, preferred_element_type=jnp.float32)
    target = picked * band_size + jnp.arange(count, dtype=jnp.int32)
    top = jnp.max(logits, axis=2)
    total = jnp.sum(jnp.exp(logits - top[:, :, None]), axis=2)
    hits = pair_ids[None, :] == target[:, None]
    found = jnp.sum(jnp.where(hits[None], logits, 0.0), axis=2)
    row_max = top
    row_sum = total
    row_pos = found
    new_max = jnp.maximum(col_max, jnp.max(logits, axis=1))
    col_sum = jnp.sum(jnp.exp(logits - new_max[:, None, :]), axis=1)
    row_max, row_sum, row_pos, col_max, col_sum = (row_max, row_sum, row_pos, new_max, col_sum)
    column_lse = col_max + jnp.log(col_sum)
    row_max, row_sum, row_pos = joined_all((row_max, row_sum, row_pos), WIDE_NARROW, join_rows)
    losses = row_max + jnp.log(row_sum) - row_pos
    learnability = lax.dynamic_slice_in_dim(losses[0] - losses[1], position * rows, rows, 0)
    return (learnability, column_lse)


def solution(mesh):
    split = Mesh(
        mesh.devices.reshape(4, 4, 2, 2, 2), ("wide_0", "wide_1", "wide_2", "narrow_0", "narrow_1")
    )
    placed = (P(WIDE, NARROW, None), P(WIDE_NARROW, None), P(), P(), P(), P(WIDE_NARROW), P())
    return jax.shard_map(
        per_device,
        mesh=split,
        in_specs=placed,
        out_specs=(P(NARROW), P(None, WIDE_NARROW)),
        check_vma=False,
    )
```

profile of v0, /device:TPU:1, one launch (start us, length us, event | category | flops | bytes accessed | tf_op | source)
XLA Modules:
  0.0 385.2 jit_solution(3234254604567877896)
XLA Ops:
  7.2 0.0 copy-start
  7.2 0.0 copy-start.4
  7.2 0.0 all-gather.16.cloned.1.call-start
  8.1 2.5 select_bitcast_fusion
  10.6 99.7 %fusion = bf16[24,1024]{1,0:T(8,128)(2,1)S(1)} fusion(bf16[640,1024]{1,0:T(8,128)(2,1)} %select_bitcast_fusion), kind=kCustom, calls=%all-reduce-scatter | all-reduce-scatter fusion | flops 786433 | bytes 1360384
  110.2 1.3 collective-permute-start.5
  111.5 1.3 collective-permute-start
  112.8 1.3 collective-permute-start.1
  114.1 1.3 collective-permute-start.2
  115.4 2.9 collective-permute-start.3
  118.3 0.0 collective-permute-done.5
  118.4 1.4 collective-permute-start.4
  119.8 0.0 copy-done.4
  119.8 0.6 dynamic-slice.5
  121.0 0.0 collective-permute-done
  121.0 0.0 collective-permute-done.1
  121.0 0.0 collective-permute-done.2
  121.0 0.0 collective-permute-done.3
  121.1 0.0 collective-permute-done.4
  121.1 1.0 concatenate.20
  122.1 0.6 dynamic-slice_bitcast_fusion
  122.7 0.0 all-gather.16.cloned.1.call-update
  122.7 0.0 all-gather.14.cloned.1.call-start
  122.8 93.5 %all-gather.16.cloned.1.call-done = bf16[32,20,1024]{2,1,0:T(8,128)(2,1)} async-done(((bf16[1,20,1024]{2,1,0:T(8,128)(2,1)}), bf16[32,20,1024]{2,1,0:T(8,128)(2,1)}) %all-gather.16.cloned.1.call-update) | async-done | bytes 1310736 | tf_op jit(solution)/shard_map/all_gather | solution.py:25
  216.3 3.3 reshape.115
  219.6 0.0 copy-start.2
  219.6 0.0 copy-start.5
  219.6 3.2 multiply_reduce_fusion.2
  222.8 0.0 copy-done.2
  222.8 0.0 copy-done.5
  222.9 1.3 multiply_reduce_fusion.3
  224.2 0.3 fusion.18
  224.5 1.4 pad_maximum_fusion
  225.9 0.0 all-gather.14.cloned.1.call-update
  226.0 0.0 copy-done
  226.0 0.0 copy-start.6
  226.0 4.0 %multiply_reduce_fusion = (f32[1280]{0:T(1024)S(1)}, f32[1280,768]{0,1:T(8,128)S(1)}) fusion(bf16[1280,1024]{1,0:T(8,128)(2,1)S(1)} %copy-done, bf16[2,1024,768]{2,1,0:T(8,128)(2,1)} %param.10), kind=kOutput, calls=%fused_computation.9 | convolution fusion | flops 2015230720 | bytes 8131584 | tf_op jit(solution)/shard_map/dot_general | solution.py:55
  230.0 0.0 copy-done.6
  230.0 2.4 multiply_reduce_fusion.1
  232.4 0.0 copy-start.3
  232.4 2.0 fusion.4
  234.4 0.0 copy-done.3
  234.4 0.0 copy-start.7
  234.4 3.6 broadcast_compare_fusion
  238.0 65.2 %all-gather.14.cloned.1.call-done = bf16[2,2560,768]{2,1,0:T(8,128)(2,1)} async-done(((bf16[2,640,768]{2,1,0:T(8,128)(2,1)}), bf16[2,2560,768]{2,1,0:T(8,128)(2,1)}) %all-gather.14.cloned.1.call-update) | async-done | bytes 7864336 | tf_op jit(solution)/shard_map/all_gather | solution.py:86
  303.3 0.0 copy-done.7
  303.3 19.6 %fusion.66 = (f32[2,1280]{1,0:T(2,128)S(1)}, f32[2,2560]{1,0:T(2,128)S(1)}, f32[2,2560,1280]{1,2,0:T(8,128)}) fusion(bf16[2,2560,768]{2,1,0:T(8,128)(2,1)} %all-gather.14.cloned.1.call-done, bf16[1,1280,768]{1,2,0:T(8,128)(2,1)} %get-tuple-element.29, bf16[1,1280,768]{1,2,0:T(8,128)(2,1)S(1)} %get-tuple-element.28, f32[2]{0:T(128)S(1)} %copy-done.7), kind=kOutput, calls=%fused_computation.132 | convolution fusion | flops 10087949312 | bytes 38041608 | tf_op jit(solution)/shard_map/hid,hjd->hij/dot_general | solution.py:89
  322.9 0.0 copy-start.1
  322.9 15.4 %exponential_reduce_fusion = (f32[2,1280]{1,0:T(2,128)S(1)}, f32[2,2560]{1,0:T(2,128)S(1)}, f32[2,2560]{1,0:T(2,128)S(1)}) fusion(f32[2,2560,1280]{1,2,0:T(8,128)} %get-tuple-element.25, f32[2,1280]{1,0:T(2,128)S(1)} %broadcast_maximum_fusion, pred[2560,1280]{0,1:T(8,128)(4,1)} %broadcast_compare_fusion, f32[2,2560]{1,0:T(2,128)S(1)} %get-tuple-element.6), kind=kLoop, calls=%fused_computation | loop fusion | flops 39308800 | bytes 29573120 | tf_op jit(solution)/shard_map/reduce_sum | solution.py:99
  338.3 10.5 %all-gather.6 = f32[4,6,2560]{2,1,0:T(8,128)S(1)} all-gather(f32[1,6,2560]{2,1,0:T(8,128)S(1)} %maximum_bitcast_fusion), channel_id=2, replica_groups=mesh['wide_0'=4,'wide_1'=4,'wide_2'=2,'narrow_0'=2,'narrow_1'=2] {'wide_0'}, dimensions={0}, use_global_device_ids=true | all-gather | bytes 307200 | tf_op jit(solution)/shard_map/all_gather | solution.py:36
  348.8 0.1 fusion.47
  349.0 10.2 %all-gather.7 = f32[4,6,2560]{2,1,0:T(8,128)S(1)} all-gather(f32[1,6,2560]{2,1,0:T(8,128)S(1)} %maximum_bitcast_fusion.1), channel_id=3, replica_groups=mesh['wide_0'=4,'wide_1'=4,'wide_2'=2,'narrow_0'=2,'narrow_1'=2] {'wide_1'}, dimensions={0}, use_global_device_ids=true | all-gather | bytes 307200 | tf_op jit(solution)/shard_map/all_gather | solution.py:36
  359.2 0.1 fusion.37
  359.4 5.5 %all-gather.8 = f32[2,6,2560]{2,1,0:T(8,128)S(1)} all-gather(f32[1,6,2560]{2,1,0:T(8,128)S(1)} %maximum_bitcast_fusion.2), channel_id=4, replica_groups=mesh['wide_0'=4,'wide_1'=4,'wide_2'=2,'narrow_0'=2,'narrow_1'=2] {'wide_2'}, dimensions={0}, use_global_device_ids=true | all-gather | bytes 184320 | tf_op jit(solution)/shard_map/all_gather | solution.py:36
  365.0 4.8 %all-gather.9 = f32[2,6,2560]{2,1,0:T(8,128)S(1)} all-gather(f32[1,6,2560]{2,1,0:T(8,128)S(1)} %maximum_bitcast_fusion.3), channel_id=5, replica_groups=mesh['wide_0'=4,'wide_1'=4,'wide_2'=2,'narrow_0'=2,'narrow_1'=2] {'narro..., dimensions={0}, use_global_device_ids=true | all-gather | bytes 184320 | tf_op jit(solution)/shard_map/all_gather | solution.py:36
  369.8 0.6 log_add_fusion
  370.5 7.2 %all-gather.10 = f32[2,6,2560]{2,1,0:T(8,128)S(1)} all-gather(f32[1,6,2560]{2,1,0:T(8,128)S(1)} %maximum_bitcast_fusion.4), channel_id=6, replica_groups=mesh['wide_0'=4,'wide_1'=4,'wide_2'=2,'narrow_0'=2,'narrow_1'=2] {'narro..., dimensions={0}, use_global_device_ids=true | all-gather | bytes 184320 | tf_op jit(solution)/shard_map/all_gather | solution.py:36
  377.7 0.1 fusion.21
  377.8 0.6 fusion.64
  378.4 0.0 copy-done.1
  (19 shorter events, 0.4 us)
Async XLA Ops:
  7.2 218.8 %copy-start = (bf16[1280,1024]{1,0:T(8,128)(2,1)S(1)}, bf16[1280,1024]{1,0:T(8,128)(2,1)}, u32[]{:S(2)}) copy-start(bf16[1280,1024]{1,0:T(8,128)(2,1)} %param.8) | copy-start | bytes 7864324
  7.2 112.6 %copy-start.4 = (u32[128]{0:T(128)S(1)}, u32[128]{0:T(128)}, u32[]{:S(2)}) copy-start(u32[128]{0:T(128)} %constant.68) | copy-start | bytes 1540
  7.2 209.1 %all-gather.16.cloned.1.call-start = ((), (), s32[]{:S(2)}) async-start(), calls=%async_computation.1 | async-start | bytes 1622016 | tf_op jit(solution)/shard_map/all_gather | solution.py:25
  110.2 8.1 %collective-permute-start.5 = (bf16[4,1024]{1,0:T(4,128)(2,1)S(1)}, bf16[4,1024]{1,0:T(4,128)(2,1)S(1)}, u32[]{:S(2)}, u32[]{:S(2)}) collective-permute-start(bf16[4,1024]{1,0:T(4,128)(2,1)S(1)} %slice.293), channel_id=1, source_target_pairs={{0,24},{4,28},{8,32},{12,36},{16,40},{20,44},{24,48},{28,52},{32,5... | collective-permute-start | bytes 24584
  111.5 9.5 %collective-permute-start = (bf16[24,1024]{1,0:T(8,128)(2,1)S(1)}, bf16[24,1024]{1,0:T(8,128)(2,1)S(1)}, u32[]{:S(2)}, u32[]{:S(2)}) collective-permute-start(bf16[24,1024]{1,0:T(8,128)(2,1)S(1)} %fusion), channel_id=1, source_target_pairs={{0,4},{4,8},{8,12},{12,16},{16,20},{20,24},{24,28},{28,32},{32,36}... | collective-permute-start | bytes 147464
  112.8 8.2 %collective-permute-start.1 = (bf16[24,1024]{1,0:T(8,128)(2,1)S(1)}, bf16[24,1024]{1,0:T(8,128)(2,1)S(1)}, u32[]{:S(2)}, u32[]{:S(2)}) collective-permute-start(bf16[24,1024]{1,0:T(8,128)(2,1)S(1)} %fusion), channel_id=1, source_target_pairs={{0,8},{4,12},{8,16},{12,20},{16,24},{20,28},{24,32},{28,36},{32,40... | collective-permute-start | bytes 147464
  114.1 6.9 %collective-permute-start.2 = (bf16[24,1024]{1,0:T(8,128)(2,1)S(1)}, bf16[24,1024]{1,0:T(8,128)(2,1)S(1)}, u32[]{:S(2)}, u32[]{:S(2)}) collective-permute-start(bf16[24,1024]{1,0:T(8,128)(2,1)S(1)} %fusion), channel_id=1, source_target_pairs={{0,12},{4,16},{8,20},{12,24},{16,28},{20,32},{24,36},{28,40},{32,4... | collective-permute-start | bytes 147464
  115.4 5.6 %collective-permute-start.3 = (bf16[24,1024]{1,0:T(8,128)(2,1)S(1)}, bf16[24,1024]{1,0:T(8,128)(2,1)S(1)}, u32[]{:S(2)}, u32[]{:S(2)}) collective-permute-start(bf16[24,1024]{1,0:T(8,128)(2,1)S(1)} %fusion), channel_id=1, source_target_pairs={{0,16},{4,20},{8,24},{12,28},{16,32},{20,36},{24,40},{28,44},{32,4... | collective-permute-start | bytes 147464
  118.4 2.7 collective-permute-start.4
  122.7 180.5 %all-gather.14.cloned.1.call-start = ((), (), s32[]{:S(2)}) async-start(), calls=%async_computation | async-start | bytes 9830400 | tf_op jit(solution)/shard_map/all_gather | solution.py:86
  219.6 3.2 copy-start.2
  219.6 3.3 copy-start.5
  226.0 4.0 %copy-start.6 = (bf16[2,1024,768]{2,1,0:T(8,128)(2,1)S(1)}, bf16[2,1024,768]{2,1,0:T(8,128)(2,1)}, u32[]{:S(2)}) copy-start(bf16[2,1024,768]{2,1,0:T(8,128)(2,1)} %param.10) | copy-start | bytes 9437188
  232.4 2.0 copy-start.3
  234.4 68.8 %copy-start.7 = (f32[2]{0:T(128)S(1)}, f32[2]{0:T(128)}, u32[]{:S(2)}) copy-start(f32[2]{0:T(128)} %param.11) | copy-start | bytes 28
  322.9 55.5 %copy-start.1 = (bf16[1280,1024]{1,0:T(8,128)(2,1)S(1)}, bf16[1280,1024]{1,0:T(8,128)(2,1)}, u32[]{:S(2)}) copy-start(bf16[1280,1024]{1,0:T(8,128)(2,1)} %param.8) | copy-start | bytes 7864324
Sparse Core Ops, SparseCore 0:
  122.9 93.4 all-gather.15
  226.1 77.1 all-gather.13
where the time goes:
time: 386 us; the launch traced here: 385 us
  waiting for transfers between devices  159 us (41%)
  blocking collectives  138 us (36%)
  matrix products  30.5 us (8%)
  other arithmetic  27.1 us (7%)
  between operations  15.9 us (4%)
  starting transfers between devices  9.55 us (2%)
  local copies, waits for them, and re-layouts  5.57 us (1%)
    unnamed x1, blocking collectives  99.7 us
    all_gather x1, waiting for transfers between devices, from_root(): lax.all_gather(own, axis, axis=0, tiled=True)[:len(lines)]  93.5 us
    all_gather x1, waiting for transfers between devices, per_device(): piece = lax.all_gather(band_emb, NARROW, axis=1, tiled=True)  65.2 us
    all_gather x5, blocking collectives, collected_together(): both, at, found = (lax.all_gather(jnp.concatenate(lines), axis), 0, {})  38.1 us
    dot_general x1, matrix products, per_device(): jnp.einsum('hid,hjd->hij', piece, text_emb, preferred_element_type=jnp.fl...  19.6 us
    reduce_sum x1, other arithmetic, per_device(): col_sum = jnp.sum(jnp.exp(logits - new_max[:, None, :]), axis=1)  15.4 us
    dot_general x4, matrix products, embed(): full = jnp.dot(tower, weight, preferred_element_type=jnp.float32)  10.9 us
    unnamed x6, starting transfers between devices  9.47 us
  transfers between devices with their start and end apart: 8, of which 2 were waited for; matrix products, arithmetic and copies ran while one was open for 3% of the time, Pallas kernels for 0%

commit v1 on v0

--- a/solution.py
+++ b/solution.py
@@ -22,7 +22,9 @@
     )
     padded = filled_up(lines, lax.axis_size(axis))
     own = lax.psum_scatter(padded, axis, scatter_dimension=0, tiled=True)
-    return lax.all_gather(own, axis, axis=0, tiled=True)[: len(lines)].reshape(value.shape)
+    return jnp.concatenate(
+        lax.all_to_all(jnp.stack([own] * lax.axis_size(axis)), axis, 0, 0), axis=0
+    )[: len(lines)].reshape(value.shape)
 
 
 def collected_together(value, axis):

time: 386 us -> 341 us (0.88)
  waiting for transfers between devices: 159 us -> 80 us
  blocking collectives: 138 us -> 173 us
    all_gather x1 -> x0, waiting for transfers between devices: 93.5 us -> none  [from_root(): lax.all_gather(own, axis, axis=0, tiled=True)[:len(lines)]]
    all_to_all x0 -> x1, blocking collectives: none -> 34.8 us  [from_root(): lax.all_to_all(jnp.stack([own] * lax.axis_size(axis)), axis, 0, 0)]
    all_gather x1, waiting for transfers between devices: 65.2 us -> 79.9 us  [per_device(): piece = lax.all_gather(band_emb, NARROW, axis=1, tiled=True)]
    unnamed x21 -> x20, local copies, waits for them, and re-layouts: 5.55 us -> 1.66 us
  transfers between devices with their start and end apart: 8 -> 7, of which waited for: 2 -> 1; matrix products, arithmetic and copies ran while one was open for 3% -> 4% of each run, Pallas kernels for 0% -> 0%
where the time goes in v1:
time: 341 us
  blocking collectives  173 us (51%)
  waiting for transfers between devices  80 us (23%)
  matrix products  30.5 us (9%)
  other arithmetic  27.1 us (8%)
  between operations  15.9 us (5%)
  starting transfers between devices  9.51 us (3%)
  local copies, waits for them, and re-layouts  5.13 us (2%)
    unnamed x1, blocking collectives  99.7 us
    all_gather x1, waiting for transfers between devices, per_device(): piece = lax.all_gather(band_emb, NARROW, axis=1, tiled=True)  79.9 us
    all_gather x5, blocking collectives, collected_together(): both, at, found = (lax.all_gather(jnp.concatenate(lines), axis), 0, {})  38.1 us
    all_to_all x1, blocking collectives, from_root(): lax.all_to_all(jnp.stack([own] * lax.axis_size(axis)), axis, 0, 0)  34.8 us
    dot_general x1, matrix products, per_device(): jnp.einsum('hid,hjd->hij', piece, text_emb, preferred_element_type=jnp.fl...  19.6 us
    reduce_sum x1, other arithmetic, per_device(): col_sum = jnp.sum(jnp.exp(logits - new_max[:, None, :]), axis=1)  15.3 us
    dot_general x4, matrix products, embed(): full = jnp.dot(tower, weight, preferred_element_type=jnp.float32)  10.9 us
    unnamed x6, starting transfers between devices  9.47 us
  transfers between devices with their start and end apart: 7, of which 1 were waited for; matrix products, arithmetic and copies ran while one was open for 4% of the time, Pallas kernels for 0%

profile of v1, /device:TPU:1, one launch (start us, length us, event | category | flops | bytes accessed | tf_op | source)
XLA Modules:
  0.0 340.6 jit_solution(4437588928815566906)
XLA Ops:
  7.2 0.0 copy-start
  7.2 0.0 copy-start.4
  7.2 0.0 all-gather.12.cloned.1.call-start
  8.1 2.5 select_bitcast_fusion
  10.5 99.7 %fusion = bf16[24,1024]{1,0:T(8,128)(2,1)S(1)} fusion(bf16[640,1024]{1,0:T(8,128)(2,1)} %select_bitcast_fusion), kind=kCustom, calls=%all-reduce-scatter | all-reduce-scatter fusion | flops 786433 | bytes 1360384
  110.2 1.3 collective-permute-start.5
  111.5 1.3 collective-permute-start
  112.8 1.3 collective-permute-start.1
  114.1 1.3 collective-permute-start.2
  115.4 2.9 collective-permute-start.3
  118.3 0.0 collective-permute-done.5
  118.3 1.4 collective-permute-start.4
  119.8 0.0 copy-done.4
  119.8 0.6 dynamic-slice.5
  121.0 0.0 collective-permute-done
  121.0 0.0 collective-permute-done.1
  121.0 0.0 collective-permute-done.2
  121.0 0.0 collective-permute-done.3
  121.0 0.0 collective-permute-done.4
  121.1 1.0 concatenate.20
  122.1 0.2 stack.14
  122.3 34.8 %all_to_all.5 = bf16[32,20,1024]{2,1,0:T(8,128)(2,1)} all-to-all(bf16[32,20,1024]{2,1,0:T(8,128)(2,1)S(1)} %stack.14), channel_id=1, replica_groups=mesh['wide_0'=4,'wide_1'=4,'wide_2'=2,'narrow_0'=2,'narrow_1'=2] {'wide_..., dimensions={0} | all-to-all | bytes 2621440 | tf_op jit(solution)/shard_map/all_to_all | solution.py:26
  157.1 3.3 reshape.114
  160.3 0.0 copy-start.2
  160.4 0.0 copy-start.5
  160.4 3.2 multiply_reduce_fusion.2
  163.6 0.0 copy-done.2
  163.6 0.0 copy-done.5
  163.6 1.3 multiply_reduce_fusion.3
  164.9 0.3 fusion.18
  165.2 1.5 pad_maximum_fusion
  166.7 0.0 all-gather.12.cloned.1.call-update
  166.7 0.0 copy-done
  166.7 0.0 copy-start.6
  166.7 4.0 %multiply_reduce_fusion = (f32[1280]{0:T(1024)S(1)}, f32[1280,768]{0,1:T(8,128)S(1)}) fusion(bf16[1280,1024]{1,0:T(8,128)(2,1)S(1)} %copy-done, bf16[2,1024,768]{2,1,0:T(8,128)(2,1)} %param.10), kind=kOutput, calls=%fused_computation.9 | convolution fusion | flops 2015230720 | bytes 8131584 | tf_op jit(solution)/shard_map/dot_general | solution.py:57
  170.7 0.0 copy-done.6
  170.7 2.4 multiply_reduce_fusion.1
  173.2 0.0 copy-start.3
  173.2 2.0 fusion.4
  175.2 0.0 copy-done.3
  175.2 0.0 copy-start.7
  175.2 3.6 %broadcast_compare_fusion = pred[2560,1280]{0,1:T(8,128)(4,1)} fusion(s32[2560]{0:T(1024)S(1)} %iota_add_fusion, s32[1280]{0:T(1024)S(1)} %copy-done.3), kind=kLoop, calls=%fused_computation.4 | loop fusion | flops 3276800 | bytes 3292160 | tf_op jit(solution)/shard_map/eq | solution.py:95
  178.8 79.9 %all-gather.12.cloned.1.call-done = bf16[2,2560,768]{2,1,0:T(8,128)(2,1)} async-done(((bf16[2,640,768]{2,1,0:T(8,128)(2,1)}), bf16[2,2560,768]{2,1,0:T(8,128)(2,1)}) %all-gather.12.cloned.1.call-update) | async-done | bytes 7864336 | tf_op jit(solution)/shard_map/all_gather | solution.py:88
  258.7 0.0 copy-done.7
  258.7 19.6 %fusion.66 = (f32[2,1280]{1,0:T(2,128)S(1)}, f32[2,2560]{1,0:T(2,128)S(1)}, f32[2,2560,1280]{1,2,0:T(8,128)}) fusion(bf16[2,2560,768]{2,1,0:T(8,128)(2,1)} %all-gather.12.cloned.1.call-done, bf16[1,1280,768]{1,2,0:T(8,128)(2,1)} %get-tuple-element.29, bf16[1,1280,768]{1,2,0:T(8,128)(2,1)S(1)} %get-tuple-element.28, f32[2]{0:T(128)S(1)} %copy-done.7), kind=kOutput, calls=%fused_computation.132 | convolution fusion | flops 10087949312 | bytes 38041608 | tf_op jit(solution)/shard_map/hid,hjd->hij/dot_general | solution.py:91
  278.3 0.0 copy-start.1
  278.4 15.3 %exponential_reduce_fusion = (f32[2,1280]{1,0:T(2,128)S(1)}, f32[2,2560]{1,0:T(2,128)S(1)}, f32[2,2560]{1,0:T(2,128)S(1)}) fusion(f32[2,2560,1280]{1,2,0:T(8,128)} %get-tuple-element.25, f32[2,1280]{1,0:T(2,128)S(1)} %broadcast_maximum_fusion, pred[2560,1280]{0,1:T(8,128)(4,1)} %broadcast_compare_fusion, f32[2,2560]{1,0:T(2,128)S(1)} %get-tuple-element.6), kind=kLoop, calls=%fused_computation | loop fusion | flops 39308800 | bytes 29573120 | tf_op jit(solution)/shard_map/reduce_sum | solution.py:101
  293.7 10.5 %all-gather.5 = f32[4,6,2560]{2,1,0:T(8,128)S(1)} all-gather(f32[1,6,2560]{2,1,0:T(8,128)S(1)} %maximum_bitcast_fusion), channel_id=2, replica_groups=mesh['wide_0'=4,'wide_1'=4,'wide_2'=2,'narrow_0'=2,'narrow_1'=2] {'wide_0'}, dimensions={0}, use_global_device_ids=true | all-gather | bytes 307200 | tf_op jit(solution)/shard_map/all_gather | solution.py:38
  304.2 0.1 fusion.47
  304.4 10.2 %all-gather.6 = f32[4,6,2560]{2,1,0:T(8,128)S(1)} all-gather(f32[1,6,2560]{2,1,0:T(8,128)S(1)} %maximum_bitcast_fusion.1), channel_id=3, replica_groups=mesh['wide_0'=4,'wide_1'=4,'wide_2'=2,'narrow_0'=2,'narrow_1'=2] {'wide_1'}, dimensions={0}, use_global_device_ids=true | all-gather | bytes 307200 | tf_op jit(solution)/shard_map/all_gather | solution.py:38
  314.6 0.1 fusion.37
  314.8 5.5 %all-gather.7 = f32[2,6,2560]{2,1,0:T(8,128)S(1)} all-gather(f32[1,6,2560]{2,1,0:T(8,128)S(1)} %maximum_bitcast_fusion.2), channel_id=4, replica_groups=mesh['wide_0'=4,'wide_1'=4,'wide_2'=2,'narrow_0'=2,'narrow_1'=2] {'wide_2'}, dimensions={0}, use_global_device_ids=true | all-gather | bytes 184320 | tf_op jit(solution)/shard_map/all_gather | solution.py:38
  320.4 4.8 %all-gather.8 = f32[2,6,2560]{2,1,0:T(8,128)S(1)} all-gather(f32[1,6,2560]{2,1,0:T(8,128)S(1)} %maximum_bitcast_fusion.3), channel_id=5, replica_groups=mesh['wide_0'=4,'wide_1'=4,'wide_2'=2,'narrow_0'=2,'narrow_1'=2] {'narro..., dimensions={0}, use_global_device_ids=true | all-gather | bytes 184320 | tf_op jit(solution)/shard_map/all_gather | solution.py:38
  325.2 0.6 log_add_fusion
  325.9 7.2 %all-gather.9 = f32[2,6,2560]{2,1,0:T(8,128)S(1)} all-gather(f32[1,6,2560]{2,1,0:T(8,128)S(1)} %maximum_bitcast_fusion.4), channel_id=6, replica_groups=mesh['wide_0'=4,'wide_1'=4,'wide_2'=2,'narrow_0'=2,'narrow_1'=2] {'narro..., dimensions={0}, use_global_device_ids=true | all-gather | bytes 184320 | tf_op jit(solution)/shard_map/all_gather | solution.py:38
  333.1 0.1 fusion.21
  333.2 0.6 fusion.64
  333.8 0.0 copy-done.1
  (20 shorter events, 0.5 us)
Async XLA Ops:
  7.2 159.6 %copy-start = (bf16[1280,1024]{1,0:T(8,128)(2,1)S(1)}, bf16[1280,1024]{1,0:T(8,128)(2,1)}, u32[]{:S(2)}) copy-start(bf16[1280,1024]{1,0:T(8,128)(2,1)} %param.8) | copy-start | bytes 7864324
  7.2 112.6 %copy-start.4 = (u32[128]{0:T(128)S(1)}, u32[128]{0:T(128)}, u32[]{:S(2)}) copy-start(u32[128]{0:T(128)} %constant.68) | copy-start | bytes 1540
  7.2 251.5 %all-gather.12.cloned.1.call-start = ((), (), s32[]{:S(2)}) async-start(), calls=%async_computation.1 | async-start | bytes 9830400 | tf_op jit(solution)/shard_map/all_gather | solution.py:88
  110.2 8.1 %collective-permute-start.5 = (bf16[4,1024]{1,0:T(4,128)(2,1)S(1)}, bf16[4,1024]{1,0:T(4,128)(2,1)S(1)}, u32[]{:S(2)}, u32[]{:S(2)}) collective-permute-start(bf16[4,1024]{1,0:T(4,128)(2,1)S(1)} %slice.293), channel_id=1, source_target_pairs={{0,24},{4,28},{8,32},{12,36},{16,40},{20,44},{24,48},{28,52},{32,5... | collective-permute-start | bytes 24584
  111.5 9.5 %collective-permute-start = (bf16[24,1024]{1,0:T(8,128)(2,1)S(1)}, bf16[24,1024]{1,0:T(8,128)(2,1)S(1)}, u32[]{:S(2)}, u32[]{:S(2)}) collective-permute-start(bf16[24,1024]{1,0:T(8,128)(2,1)S(1)} %fusion), channel_id=1, source_target_pairs={{0,4},{4,8},{8,12},{12,16},{16,20},{20,24},{24,28},{28,32},{32,36}... | collective-permute-start | bytes 147464
  112.8 8.2 %collective-permute-start.1 = (bf16[24,1024]{1,0:T(8,128)(2,1)S(1)}, bf16[24,1024]{1,0:T(8,128)(2,1)S(1)}, u32[]{:S(2)}, u32[]{:S(2)}) collective-permute-start(bf16[24,1024]{1,0:T(8,128)(2,1)S(1)} %fusion), channel_id=1, source_target_pairs={{0,8},{4,12},{8,16},{12,20},{16,24},{20,28},{24,32},{28,36},{32,40... | collective-permute-start | bytes 147464
  114.1 6.9 %collective-permute-start.2 = (bf16[24,1024]{1,0:T(8,128)(2,1)S(1)}, bf16[24,1024]{1,0:T(8,128)(2,1)S(1)}, u32[]{:S(2)}, u32[]{:S(2)}) collective-permute-start(bf16[24,1024]{1,0:T(8,128)(2,1)S(1)} %fusion), channel_id=1, source_target_pairs={{0,12},{4,16},{8,20},{12,24},{16,28},{20,32},{24,36},{28,40},{32,4... | collective-permute-start | bytes 147464
  115.4 5.6 %collective-permute-start.3 = (bf16[24,1024]{1,0:T(8,128)(2,1)S(1)}, bf16[24,1024]{1,0:T(8,128)(2,1)S(1)}, u32[]{:S(2)}, u32[]{:S(2)}) collective-permute-start(bf16[24,1024]{1,0:T(8,128)(2,1)S(1)} %fusion), channel_id=1, source_target_pairs={{0,16},{4,20},{8,24},{12,28},{16,32},{20,36},{24,40},{28,44},{32,4... | collective-permute-start | bytes 147464
  118.3 2.7 collective-permute-start.4
  160.3 3.2 copy-start.2
  160.4 3.3 copy-start.5
  166.7 4.0 %copy-start.6 = (bf16[2,1024,768]{2,1,0:T(8,128)(2,1)S(1)}, bf16[2,1024,768]{2,1,0:T(8,128)(2,1)}, u32[]{:S(2)}) copy-start(bf16[2,1024,768]{2,1,0:T(8,128)(2,1)} %param.10) | copy-start | bytes 9437188
  173.2 2.0 copy-start.3
  175.2 83.5 %copy-start.7 = (f32[2]{0:T(128)S(1)}, f32[2]{0:T(128)}, u32[]{:S(2)}) copy-start(f32[2]{0:T(128)} %param.11) | copy-start | bytes 28
  278.3 55.5 %copy-start.1 = (bf16[1280,1024]{1,0:T(8,128)(2,1)S(1)}, bf16[1280,1024]{1,0:T(8,128)(2,1)}, u32[]{:S(2)}) copy-start(bf16[1280,1024]{1,0:T(8,128)(2,1)} %param.8) | copy-start | bytes 7864324
Sparse Core Ops, SparseCore 0:
  166.8 91.8 all-gather.11
